TPU v7x, 32 devices: a whole 2x2x4 slice. The times are simulated.
32 devices in a mesh: gx: 2 (over x), gy: 4 (over z), gz: 4 (over y, core).
Axes of the slice: x: 2, y: 2, z: 4, core: 2. Of those that a mesh axis runs over, the one named last changes fastest.
Arguments:
- vectors: float32 [3, 12, 24, 24, 128], P(None, 'gx', 'gy', 'gz'), may hold values from -6 to 6
- orient_flip: int32 [4, 8, 1152], P('gx', 'gy', 'gz'), may hold values from 0 to 1
- reluctivity: float32 [4, 8, 512], P('gx', 'gy', 'gz'), may hold values from 0.05 to 0.5
- conductivity: float32 [4, 8, 512], P('gx', 'gy', 'gz'), may hold values from 1 to 10
Outputs:
- out_x: float32 [12, 28, 28, 128], P('gx', 'gy', 'gz')
- out_y: float32 [14, 24, 28, 128], P('gx', 'gy', 'gz')
- out_z: float32 [14, 28, 24, 128], P('gx', 'gy', 'gz')
Inputs may be any that keep to these rules, and one draw needn't show every extreme that they name: `orient_flip`: 1 reverses the orientation of that degree of freedom in that element, 0 keeps it.
All inputs are finite; a program needn't handle non-finite values.
Results may differ from a plain program's by a relative error of at most 0.00007.
Values sent between devices are 32-bit elements; how exact they have to be, the bound alone decides.
A program may use at most 64 MiB of HBM per device.

v0:
```python
import functools
import jax
import jax.numpy as jnp
import numpy as np
from jax import lax
from jax.experimental import pallas as pl
from jax.experimental.pallas import tpu as pltpu
from jax.sharding import PartitionSpec as P

ORDER = 3
QUAD = 4
ELEM_DOFS = 144
QPTS = 64
AXES = ("gx", "gy", "gz")
MESH = pl.DeviceIdType.MESH


def lagrange(points_at, evaluate_at):
    amount = len(points_at)
    values = np.ones((len(evaluate_at), amount))
    slopes = np.zeros((len(evaluate_at), amount))
    for which in range(amount):
        for column in range(amount):
            if column != which:
                factor = (evaluate_at - points_at[column]) / (points_at[which] - points_at[column])
                slopes[:, which] = slopes[:, which] * factor + values[:, which] / (
                    points_at[which] - points_at[column]
                )
                values[:, which] = values[:, which] * factor
    return (values, slopes)


def basis_tables():
    lobatto = np.array([0.0, (1 - 5 ** (-0.5)) / 2, (1 + 5 ** (-0.5)) / 2, 1.0])
    gauss_open = np.array([(1 - 0.6**0.5) / 2, 0.5, (1 + 0.6**0.5) / 2])
    inner_pt = (3.0 / 7 - 2.0 / 7 * (6.0 / 5) ** 0.5) ** 0.5
    outer_pt = (3.0 / 7 + 2.0 / 7 * (6.0 / 5) ** 0.5) ** 0.5
    inner_wt = (18 + 30**0.5) / 36
    outer_wt = (18 - 30**0.5) / 36
    quad_points = (1 + np.array([-outer_pt, -inner_pt, inner_pt, outer_pt])) / 2
    quad_weight = np.array([outer_wt, inner_wt, inner_wt, outer_wt]) / 2
    closed, _ = lagrange(lobatto, quad_points)
    opened, _ = lagrange(gauss_open, quad_points)
    _, colloc = lagrange(quad_points, quad_points)
    return closed, opened, colloc, quad_weight


CLOSED, OPENED, COLLOC, WEIGHT = basis_tables()


def add_all(terms):
    total = terms[0]
    for term in terms[1:]:
        total = total + term
    return total


def apply(mat, xs, sigma=1):
    rows, cols = mat.shape
    half = cols // 2
    plus = [xs[p] + xs[cols - 1 - p] for p in range(half)]
    minus = [xs[p] - xs[cols - 1 - p] for p in range(half)]
    ys = [None] * rows
    for q in range((rows + 1) // 2):
        even_c = [(mat[q, p] + mat[q, cols - 1 - p]) / 2 for p in range(half)]
        odd_c = [(mat[q, p] - mat[q, cols - 1 - p]) / 2 for p in range(half)]
        even = [np.float32(c) * s for c, s in zip(even_c, plus)]
        if cols % 2:
            even.append(np.float32(mat[q, half]) * xs[half])
        even = add_all(even)
        if 2 * q == rows - 1:
            ys[q] = even
            continue
        odd = add_all([np.float32(c) * d for c, d in zip(odd_c, minus)])
        ys[q] = even + odd
        ys[rows - 1 - q] = even - odd if sigma > 0 else odd - even
    return ys


def swap(blocks, size):
    count = blocks[0].shape[0] // size
    return [
        jnp.concatenate([b[q * size : (q + 1) * size] for b in blocks], 0) for q in range(count)
    ]


def dims_of(comp):
    return [ORDER if axis == comp else ORDER + 1 for axis in range(3)]


def kernel(
    mesh_sizes, vec, flip, reluct, conduct, out_x, out_y, out_z,
    elem, sign, mass, curlw, flat, tmp, uq, cq,
    res_x, res_y, res_z, pack1, corner1, hx, hy, hz, hc, pack2_x, pack2_y, corner2,
    rim_xy, rim_xz, rim_yx, rim_yz, rim_zx, rim_zy, rc,
    s1, r1, s2, r2,
):
    f32 = jnp.float32
    cx, cy = flip.shape[0], flip.shape[1]
    cz = flip.shape[2] // ELEM_DOFS
    counts = (cx, cy, cz)
    ne = cx * cy * cz
    size = tuple(ORDER * c for c in counts)
    me = [lax.axis_index(a) for a in AXES]

    def device(shift):
        return tuple(
            lax.rem(me[a] + (shift[a] + mesh_sizes[a]), mesh_sizes[a]) for a in range(3)
        )

    offsets = []
    for dx in (-1, 0, 1):
        for dy in (-1, 0, 1):
            for dz in (-1, 0, 1):
                if 1 <= abs(dx) + abs(dy) + abs(dz) <= 2:
                    offsets.append((dx, dy, dz))
    barrier = pltpu.get_barrier_semaphore()
    for shift in offsets:
        pl.semaphore_signal(barrier, inc=1, device_id=device(shift), device_id_type=MESH)

    for comp in (0, 1):
        for x in range(size[0]):
            for y in range(size[1]):
                pack1[comp, x, y : y + 1, :] = vec[comp, x, y, 0:1, :]
    for x in range(size[0]):
        corner1[0, x : x + 1, :] = vec[0, x, 0, 0:1, :]
    for y in range(size[1]):
        corner1[1, y : y + 1, :] = vec[1, 0, y, 0:1, :]
    pl.semaphore_wait(barrier, len(offsets))

    copies = []

    def send(src, dst, shift, sends, recvs, which):
        copy = pltpu.make_async_remote_copy(
            src_ref=src, dst_ref=dst, send_sem=sends.at[which], recv_sem=recvs.at[which],
            device_id=device(shift), device_id_type=MESH,
        )
        copy.start()
        return copy

    one = [
        send(vec.at[0, :, 0], hy.at[0], (0, -1, 0), s1, r1, 0),
        send(vec.at[2, :, 0], hy.at[1], (0, -1, 0), s1, r1, 1),
        send(vec.at[1:3, 0], hx, (-1, 0, 0), s1, r1, 2),
        send(pack1, hz, (0, 0, -1), s1, r1, 3),
        send(corner1.at[0], hc.at[0], (0, -1, -1), s1, r1, 4),
        send(corner1.at[1], hc.at[1], (-1, 0, -1), s1, r1, 5),
        send(vec.at[2, 0, 0], hc.at[2], (-1, -1, 0), s1, r1, 6),
    ]

    for i in range(cx):
        for j in range(cy):
            for k in range(cz):
                e = (i * cy + j) * cz + k
                flat[0, e : e + 1, 0:ELEM_DOFS] = 1.0 - 2.0 * flip[
                    i, j : j + 1, k * ELEM_DOFS : (k + 1) * ELEM_DOFS
                ].astype(f32)
                flat[1, e : e + 1, 0:QPTS] = reluct[i, j : j + 1, k * QPTS : (k + 1) * QPTS]
                flat[2, e : e + 1, 0:QPTS] = conduct[i, j : j + 1, k * QPTS : (k + 1) * QPTS]
    lanes = vec.shape[-1]
    for d in range(ELEM_DOFS):
        sign[d * ne : (d + 1) * ne, :] = jnp.broadcast_to(flat[0, :, d : d + 1], (ne, lanes))
    for q in range(QPTS):
        w = np.float32(WEIGHT[q // 16] * WEIGHT[q // 4 % 4] * WEIGHT[q % 4])
        rows = slice(q * ne, (q + 1) * ne)
        curlw[rows, :] = jnp.broadcast_to(flat[1, :, q : q + 1] * w, (ne, lanes))
        mass[rows, :] = jnp.broadcast_to(flat[2, :, q : q + 1] * w, (ne, lanes))

    def homes(comp, axis, low, high):
        found = []
        for el in range(counts[axis]):
            first = max(low, ORDER * el)
            last = min(high, ORDER * el + dims_of(comp)[axis])
            if first < last:
                found.append((el, first - ORDER * el, first - low, last - first))
        return found

    def places(comp, axis, at, low, high):
        dims = dims_of(comp)
        steps = (dims[1] * dims[2], dims[2], 1)
        span = [(p, p + 1) for p in at]
        span[axis] = (low, high)
        for fx in homes(comp, 0, *span[0]):
            for fy in homes(comp, 1, *span[1]):
                for fz in homes(comp, 2, *span[2]):
                    found = (fx, fy, fz)
                    e = (fx[0] * cy + fy[0]) * cz + fz[0]
                    d = comp * 48 + sum(found[t][1] * steps[t] for t in range(3))
                    yield found[axis][2], found[axis][3], d * ne + e, steps[axis] * ne

    def put(comp, axis, at, low, high, load):
        for offset, length, row, stride in places(comp, axis, at, low, high):
            elem[pl.ds(row, length, stride=stride), :] = load(offset, offset + length)

    for comp in range(3):
        for x in range(size[0]):
            for y in range(size[1]):
                put(comp, 2, (x, y, 0), 0, size[2], lambda a, b: vec[comp, x, y, a:b, :])

    for copy in one:
        copy.wait_recv()
    for slot, comp in ((0, 0), (1, 2)):
        for x in range(size[0]):
            put(comp, 2, (x, size[1], 0), 0, size[2], lambda a, b: hy[slot, x, a:b, :])
    for slot, comp in ((0, 1), (1, 2)):
        for y in range(size[1]):
            put(comp, 2, (size[0], y, 0), 0, size[2], lambda a, b: hx[slot, y, a:b, :])
    for comp in (0, 1):
        for x in range(size[0]):
            put(comp, 1, (x, 0, size[2]), 0, size[1], lambda a, b: hz[comp, x, a:b, :])
    put(0, 0, (0, size[1], size[2]), 0, size[0], lambda a, b: hc[0, a:b, :])
    put(1, 1, (size[0], 0, size[2]), 0, size[1], lambda a, b: hc[1, a:b, :])
    put(2, 2, (size[0], size[1], 0), 0, size[2], lambda a, b: hc[2, a:b, :])

    def rows_of(axis, at, line, dims):
        others = [t for t in range(3) if t != axis]
        points = []
        for last in range(dims[others[1]]):
            index = [0, 0, 0]
            index[axis], index[others[0]], index[others[1]] = at, line, last
            points.append(((index[0] * dims[1] + index[1]) * dims[2] + index[2]) * ne)
        return points

    def load_line(ref, base, axis, at, line, dims):
        starts = [base + r for r in rows_of(axis, at, line, dims)]
        if len(starts) > 1 and starts[1] - starts[0] == ne:
            return ref[starts[0] : starts[-1] + ne, :]
        return jnp.concatenate([ref[s : s + ne, :] for s in starts], 0)

    def load_plane(ref, base, axis, at, dims):
        others = [t for t in range(3) if t != axis]
        return [load_line(ref, base, axis, at, p, dims) for p in range(dims[others[0]])]

    def store_plane(ref, base, axis, at, dims, blocks):
        for p, block in enumerate(blocks):
            starts = [base + r for r in rows_of(axis, at, p, dims)]
            if starts[1] - starts[0] == ne:
                ref[starts[0] : starts[-1] + ne, :] = block
            else:
                for t, s in enumerate(starts):
                    ref[s : s + ne, :] = block[t * ne : (t + 1) * ne]

    full = [QUAD] * 3

    def mid_dims(comp):
        return [ORDER if axis == comp else QUAD for axis in range(3)]

    for comp in range(3):
        dims = dims_of(comp)
        base = comp * 48 * ne
        for a in range(ORDER):
            plane = load_plane(elem, base, comp, a, dims)
            signs = load_plane(sign, base, comp, a, dims)
            plane = [p * s for p, s in zip(plane, signs)]
            plane = apply(CLOSED, plane)
            plane = apply(CLOSED, swap(plane, ne))
            store_plane(tmp, base, comp, a, mid_dims(comp), swap(plane, ne))
        others = [t for t in range(3) if t != comp]
        for line in range(QUAD):
            xs = [load_line(tmp, base, comp, a, line, mid_dims(comp)) for a in range(ORDER)]
            for q, y in enumerate(apply(OPENED, xs)):
                starts = [comp * 64 * ne + r for r in rows_of(comp, q, line, full)]
                if starts[1] - starts[0] == ne:
                    uq[starts[0] : starts[-1] + ne, :] = y
                else:
                    for t, s in enumerate(starts):
                        uq[s : s + ne, :] = y[t * ne : (t + 1) * ne]

    part = 64 * ne

    for c in range(3):
        p, r = [t for t in range(3) if t != c]
        flipped = -1 if c == 1 else 1
        for at in range(QUAD):
            u_p = load_plane(uq, p * part, c, at, full)
            u_r = load_plane(uq, r * part, c, at, full)
            along_p = apply(COLLOC, u_r, -1)
            along_r = swap(apply(COLLOC, swap(u_p, ne), -1), ne)
            if flipped > 0:
                curl = [f - g for f, g in zip(along_p, along_r)]
            else:
                curl = [g - f for f, g in zip(along_p, along_r)]
            scale = load_plane(curlw, 0, c, at, full)
            store_plane(cq, c * part, c, at, full, [k * w for k, w in zip(curl, scale)])

    closed_t, opened_t, colloc_t = CLOSED.T, OPENED.T, COLLOC.T
    results = (res_x, res_y, res_z)
    packs = (pack2_x, pack2_y)
    rims = ((None, rim_xy, rim_xz), (rim_yx, None, rim_yz), (rim_zx, rim_zy, None))
    for res in results:
        res[...] = jnp.zeros_like(res)
    two = []
    for comp in range(3):
        dims = dims_of(comp)
        base = comp * 48 * ne
        p, r = [t for t in range(3) if t != comp]
        for at in range(QUAD):
            u = load_plane(uq, comp * part, comp, at, full)
            m = load_plane(mass, 0, comp, at, full)
            total = [a * b for a, b in zip(u, m)]
            by_p = apply(colloc_t, load_plane(cq, r * part, comp, at, full), -1)
            by_r = apply(colloc_t, swap(load_plane(cq, p * part, comp, at, full), ne), -1)
            by_r = swap(by_r, ne)
            if comp == 1:
                total = [t + a - b for t, a, b in zip(total, by_p, by_r)]
            else:
                total = [t - a + b for t, a, b in zip(total, by_p, by_r)]
            total = apply(closed_t, total)
            total = apply(closed_t, swap(total, ne))
            kept = [QUAD if axis == comp else ORDER + 1 for axis in range(3)]
            store_plane(tmp, 0, comp, at, kept, swap(total, ne))
        for line in range(ORDER + 1):
            xs = [load_line(tmp, 0, comp, q, line, kept) for q in range(QUAD)]
            for a, y in enumerate(apply(opened_t, xs)):
                y = y * load_line(sign, base, comp, a, line, dims)
                for t, s in enumerate(rows_of(comp, a, line, dims)):
                    elem[base + s : base + s + ne, :] = y[t * ne : (t + 1) * ne]
        res = results[comp]
        for x in range(res.shape[0]):
            for y in range(res.shape[1]):
                for offset, length, row, stride in places(comp, 2, (x, y, 0), 0, res.shape[2]):
                    res[x, y, offset : offset + length, :] += elem[
                        pl.ds(row, length, stride=stride), :
                    ]
        if comp < 2:
            for side in (0, 1):
                z = side * size[2]
                for x in range(res.shape[0]):
                    for y in range(res.shape[1]):
                        packs[comp][side, x, y : y + 1, :] = res[x, y, z : z + 1, :]
        for axis in range(3):
            if axis == comp:
                continue
            for side in (0, 1):
                shift = [0, 0, 0]
                shift[axis] = 2 * side - 1
                if axis == 0:
                    src = res.at[side * size[0]]
                elif axis == 1:
                    src = res.at[:, side * size[1]]
                else:
                    src = packs[comp].at[side]
                dst = rims[comp][axis].at[side]
                two.append(send(src, dst, shift, s2, r2, len(two)))
        for sp in (0, 1):
            for sr in (0, 1):
                shift = [0, 0, 0]
                shift[p], shift[r] = 2 * sp - 1, 2 * sr - 1
                where = 4 * comp + 2 * sp + sr
                if comp == 0:
                    for x in range(size[0]):
                        corner2[where, x : x + 1, :] = res[
                            x, sp * size[1], sr * size[2] : sr * size[2] + 1, :
                        ]
                    src = corner2.at[where]
                elif comp == 1:
                    for y in range(size[1]):
                        corner2[where, y : y + 1, :] = res[
                            sp * size[0], y, sr * size[2] : sr * size[2] + 1, :
                        ]
                    src = corner2.at[where]
                else:
                    src = res.at[sp * size[0], sr * size[1]]
                two.append(send(src, rc.at[where], shift, s2, r2, len(two)))

    outs = (out_x, out_y, out_z)
    for comp in range(3):
        outs[comp][...] = results[comp][...]
    for copy in two:
        copy.wait_recv()
    for comp in range(3):
        out = outs[comp]
        p, r = [t for t in range(3) if t != comp]
        for side in (0, 1):
            far = 1 - side
            if comp != 0:
                out[far * size[0]] += rims[comp][0][side]
            if comp != 1:
                for x in range(out.shape[0]):
                    out[x, far * size[1]] += rims[comp][1][side, x]
            if comp != 2:
                z = far * size[2]
                for x in range(out.shape[0]):
                    for y in range(out.shape[1]):
                        out[x, y, z : z + 1, :] += rims[comp][2][side, x, y : y + 1, :]
        for sp in (0, 1):
            for sr in (0, 1):
                where = 4 * comp + 2 * sp + sr
                fp, fr = (1 - sp) * size[p], (1 - sr) * size[r]
                if comp == 0:
                    for x in range(size[0]):
                        out[x, fp, fr : fr + 1, :] += rc[where, x : x + 1, :]
                elif comp == 1:
                    for y in range(size[1]):
                        out[fp, y, fr : fr + 1, :] += rc[where, y : y + 1, :]
                else:
                    out[fp, fr] += rc[where]
    for copy in one + two:
        copy.wait_send()


def on_device(mesh_sizes, vectors, orient_flip, reluctivity, conductivity):
    counts = (
        orient_flip.shape[0], orient_flip.shape[1], orient_flip.shape[2] // ELEM_DOFS,
    )
    ne = counts[0] * counts[1] * counts[2]
    sx, sy, sz = (ORDER * c for c in counts)
    lanes = vectors.shape[-1]
    f32 = jnp.float32
    shapes = (
        (sx, sy + 1, sz + 1, lanes), (sx + 1, sy, sz + 1, lanes), (sx + 1, sy + 1, sz, lanes),
    )
    longest = max(sx, sy, sz)
    scratch = [
        (ELEM_DOFS * ne, lanes), (ELEM_DOFS * ne, lanes), (QPTS * ne, lanes), (QPTS * ne, lanes),
        (3, ne, ELEM_DOFS), (ELEM_DOFS * ne, lanes), (3 * QPTS * ne, lanes), (3 * QPTS * ne, lanes),
        *shapes,
        (2, sx, sy, lanes), (2, longest, lanes),
        (2, sy, sz, lanes), (2, sx, sz, lanes), (2, sx, sy, lanes), (3, longest, lanes),
        (2, sx, sy + 1, lanes), (2, sx + 1, sy, lanes), (12, longest, lanes),
        (2, sx, sz + 1, lanes), (2, sx, sy + 1, lanes),
        (2, sy, sz + 1, lanes), (2, sx + 1, sy, lanes),
        (2, sy + 1, sz, lanes), (2, sx + 1, sz, lanes),
        (12, longest, lanes),
    ]
    vmem = pl.BlockSpec(memory_space=pltpu.VMEM)
    return tuple(
        pl.pallas_call(
            functools.partial(kernel, mesh_sizes),
            out_shape=[jax.ShapeDtypeStruct(s, f32) for s in shapes],
            in_specs=[vmem] * 4,
            out_specs=[vmem] * 3,
            scratch_shapes=[pltpu.VMEM(s, f32) for s in scratch]
            + [pltpu.SemaphoreType.DMA((7,))] * 2
            + [pltpu.SemaphoreType.DMA((24,))] * 2,
            compiler_params=pltpu.CompilerParams(
                collective_id=0, has_side_effects=True, vmem_limit_bytes=48 * 2**20
            ),
            name="curl_mass",
        )(vectors, orient_flip, reluctivity, conductivity)
    )


def solution(mesh):
    return jax.shard_map(
        functools.partial(on_device, tuple(mesh.shape[a] for a in AXES)),
        mesh=mesh,
        in_specs=(
            P(None, "gx", "gy", "gz", None),
            P("gx", "gy", "gz"),
            P("gx", "gy", "gz"),
            P("gx", "gy", "gz"),
        ),
        out_specs=(P("gx", "gy", "gz", None), P("gx", "gy", "gz", None), P("gx", "gy", "gz", None)),
        check_vma=False,
    )
```

profile of v0, /device:TPU:0, one launch (start us, length us, event | category | flops | bytes accessed | tf_op | source)
XLA Modules:
  0.0 23.7 jit_solution(7020619173078321683)
XLA Ops:
  0.6 0.0 copy-start
  0.6 1.0 %copy-done = f32[3,6,6,6,128]{4,3,2,1,0:T(8,128)S(1)} copy-done((f32[3,6,6,6,128]{4,3,2,1,0:T(8,128)S(1)}, f32[3,6,6,6,128]{4,3,2,1,0:T(8,128)}, u32[]{:S(2)}) %copy-start) | copy-done | bytes 331800
  1.6 0.0 copy-start.1
  1.6 0.7 %copy-done.1 = s32[2,2,288]{2,1,0:T(2,128)S(1)} copy-done((s32[2,2,288]{2,1,0:T(2,128)S(1)}, s32[2,2,288]{2,1,0:T(2,128)}, u32[]{:S(2)}) %copy-start.1) | copy-done | bytes 4632
  2.3 0.0 copy-start.2
  2.3 0.7 %copy-done.2 = f32[2,2,128]{2,1,0:T(2,128)S(1)} copy-done((f32[2,2,128]{2,1,0:T(2,128)S(1)}, f32[2,2,128]{2,1,0:T(2,128)}, u32[]{:S(2)}) %copy-start.2) | copy-done | bytes 2072
  3.0 0.0 copy-start.3
  3.0 0.7 %copy-done.3 = f32[2,2,128]{2,1,0:T(2,128)S(1)} copy-done((f32[2,2,128]{2,1,0:T(2,128)S(1)}, f32[2,2,128]{2,1,0:T(2,128)}, u32[]{:S(2)}) %copy-start.3) | copy-done | bytes 2072
  3.7 17.9 %curl_mass.1 = (f32[6,7,7,128]{3,2,1,0:T(8,128)S(1)}, f32[7,6,7,128]{3,2,1,0:T(8,128)S(1)}, f32[7,7,6,128]{3,2,1,0:T(8,128)S(1)}) custom-call(f32[3,6,6,6,128]{4,3,2,1,0:T(8,128)S(1)} %copy-done, s32[2,2,288]{2,1,0:T(2,128)S(1)} %copy-done.1, f32[2,2,128]{2,1,0:T(2,128)S(1)} %copy-done.2, f32[2,2,128]{2,1,0:T(2,128)S(1)} %copy-done.3), custom_call_target="tpu_custom_call" | custom-call | tf_op jit(solution)/shard_map/curl_mass/pallas_call | solution.py:428
  21.6 0.7 %copy.7 = f32[7,7,6,128]{3,1,2,0:T(8,128)} copy(f32[7,7,6,128]{3,2,1,0:T(8,128)S(1)} %get-tuple-element.5) | data formatting | bytes 301056 | tf_op jit(solution)/shard_map/curl_mass/pallas_call | solution.py:428
  22.3 0.7 %copy.10 = f32[6,7,7,128]{3,2,1,0:T(8,128)} copy(f32[6,7,7,128]{3,2,1,0:T(8,128)S(1)} %get-tuple-element.9) | data formatting | bytes 301056
  23.0 0.7 %copy.11 = f32[7,6,7,128]{3,2,1,0:T(8,128)} copy(f32[7,6,7,128]{3,2,1,0:T(8,128)S(1)} %get-tuple-element.10) | data formatting | bytes 301056
Async XLA Ops:
  0.6 1.0 %copy-start = (f32[3,6,6,6,128]{4,3,2,1,0:T(8,128)S(1)}, f32[3,6,6,6,128]{4,3,2,1,0:T(8,128)}, u32[]{:S(2)}) copy-start(f32[3,6,6,6,128]{4,3,2,1,0:T(8,128)} %vec.1) | copy-start | bytes 995332
  1.6 0.7 %copy-start.1 = (s32[2,2,288]{2,1,0:T(2,128)S(1)}, s32[2,2,288]{2,1,0:T(2,128)}, u32[]{:S(2)}) copy-start(s32[2,2,288]{2,1,0:T(2,128)} %flip.1) | copy-start | bytes 13828
  2.3 0.7 %copy-start.2 = (f32[2,2,128]{2,1,0:T(2,128)S(1)}, f32[2,2,128]{2,1,0:T(2,128)}, u32[]{:S(2)}) copy-start(f32[2,2,128]{2,1,0:T(2,128)} %reluct.1) | copy-start | bytes 6148
  3.0 0.7 %copy-start.3 = (f32[2,2,128]{2,1,0:T(2,128)S(1)}, f32[2,2,128]{2,1,0:T(2,128)}, u32[]{:S(2)}) copy-start(f32[2,2,128]{2,1,0:T(2,128)} %conduct.1) | copy-start | bytes 6148
where the time goes:
time: 23.9 us; the launch traced here: 23.7 us
  Pallas kernels  17.9 us (75%)
  local copies, waits for them, and re-layouts  5.1 us (21%)
  between operations  0.65 us (3%)
    pallas_call x1, Pallas kernels, on_device(): pl.pallas_call(functools.partial(kernel, mesh_sizes), out_shape=[jax.Shap...  17.9 us
    unnamed x10, local copies, waits for them, and re-layouts  4.4 us
    pallas_call x1, local copies, waits for them, and re-layouts, on_device(): pl.pallas_call(functools.partial(kernel, mesh_sizes), out_shape=[jax.Shap...  0.7 us

commit v1 on v0

--- a/solution.py
+++ b/solution.py
@@ -13,6 +13,7 @@
 QPTS = 64
 AXES = ("gx", "gy", "gz")
 MESH = pl.DeviceIdType.MESH
+VMEM_ALL = 67043328
 
 
 def lagrange(points_at, evaluate_at):
@@ -89,11 +90,11 @@
 
 
 def kernel(
-    mesh_sizes, vec, flip, reluct, conduct, out_x, out_y, out_z,
-    elem, sign, mass, curlw, flat, tmp, uq, cq,
-    res_x, res_y, res_z, pack1, corner1, hx, hy, hz, hc, pack2_x, pack2_y, corner2,
-    rim_xy, rim_xz, rim_yx, rim_yz, rim_zx, rim_zy, rc,
-    s1, r1, s2, r2,
+    mesh_sizes, vec_hbm, flip_hbm, reluct_hbm, conduct_hbm, out_x, out_y, out_z,
+    vec, flip, reluct, conduct, elem, sign, mass, curlw, flat, tmp, uq, cq,
+    res_x, res_y, res_z, pack1, corner1, hx, hy, hz, hc, pack2_x, pack2_y, pack2_z, corner2,
+    near_x, near_y, near_z, last_x, last_y, last_z, rc,
+    s1, r1, s2, r2, s0,
 ):
     f32 = jnp.float32
     cx, cy = flip.shape[0], flip.shape[1]
@@ -114,10 +115,19 @@
             for dz in (-1, 0, 1):
                 if 1 <= abs(dx) + abs(dy) + abs(dz) <= 2:
                     offsets.append((dx, dy, dz))
+    fetches = [
+        pltpu.make_async_copy(src, dst, s0.at[t])
+        for t, (src, dst) in enumerate(
+            ((vec_hbm, vec), (flip_hbm, flip), (reluct_hbm, reluct), (conduct_hbm, conduct))
+        )
+    ]
+    for fetch in fetches:
+        fetch.start()
     barrier = pltpu.get_barrier_semaphore()
     for shift in offsets:
         pl.semaphore_signal(barrier, inc=1, device_id=device(shift), device_id_type=MESH)
 
+    fetches[0].wait()
     for comp in (0, 1):
         for x in range(size[0]):
             for y in range(size[1]):
@@ -128,8 +138,6 @@
         corner1[1, y : y + 1, :] = vec[1, 0, y, 0:1, :]
     pl.semaphore_wait(barrier, len(offsets))
 
-    copies = []
-
     def send(src, dst, shift, sends, recvs, which):
         copy = pltpu.make_async_remote_copy(
             src_ref=src, dst_ref=dst, send_sem=sends.at[which], recv_sem=recvs.at[which],
@@ -139,15 +147,17 @@
         return copy
 
     one = [
+        send(corner1.at[0], hc.at[0], (0, -1, -1), s1, r1, 4),
+        send(vec.at[2, 0, 0], hc.at[2], (-1, -1, 0), s1, r1, 6),
+        send(corner1.at[1], hc.at[1], (-1, 0, -1), s1, r1, 5),
         send(vec.at[0, :, 0], hy.at[0], (0, -1, 0), s1, r1, 0),
         send(vec.at[2, :, 0], hy.at[1], (0, -1, 0), s1, r1, 1),
+        send(pack1, hz, (0, 0, -1), s1, r1, 3),
         send(vec.at[1:3, 0], hx, (-1, 0, 0), s1, r1, 2),
-        send(pack1, hz, (0, 0, -1), s1, r1, 3),
-        send(corner1.at[0], hc.at[0], (0, -1, -1), s1, r1, 4),
-        send(corner1.at[1], hc.at[1], (-1, 0, -1), s1, r1, 5),
-        send(vec.at[2, 0, 0], hc.at[2], (-1, -1, 0), s1, r1, 6),
     ]
 
+    for fetch in fetches[1:]:
+        fetch.wait()
     for i in range(cx):
         for j in range(cy):
             for k in range(cz):
@@ -285,12 +295,14 @@
 
     closed_t, opened_t, colloc_t = CLOSED.T, OPENED.T, COLLOC.T
     results = (res_x, res_y, res_z)
-    packs = (pack2_x, pack2_y)
-    rims = ((None, rim_xy, rim_xz), (rim_yx, None, rim_yz), (rim_zx, rim_zy, None))
+    packs = (pack2_x, pack2_y, pack2_z)
+    near = (near_x, near_y, near_z)
+    last = (last_x, last_y, last_z)
+    orders = ((0, 1, 2), (0, 1, 2), (0, 2, 1))
+    sends = {}
     for res in results:
         res[...] = jnp.zeros_like(res)
-    two = []
-    for comp in range(3):
+    for comp in (0, 2, 1):
         dims = dims_of(comp)
         base = comp * 48 * ne
         p, r = [t for t in range(3) if t != comp]
@@ -316,87 +328,86 @@
                 for t, s in enumerate(rows_of(comp, a, line, dims)):
                     elem[base + s : base + s + ne, :] = y[t * ne : (t + 1) * ne]
         res = results[comp]
-        for x in range(res.shape[0]):
-            for y in range(res.shape[1]):
-                for offset, length, row, stride in places(comp, 2, (x, y, 0), 0, res.shape[2]):
-                    res[x, y, offset : offset + length, :] += elem[
+        order = orders[comp]
+        for first in range(res.shape[0]):
+            for middle in range(res.shape[1]):
+                at = [0, 0, 0]
+                at[order[0]], at[order[1]] = first, middle
+                pieces = places(comp, order[2], at, 0, res.shape[2])
+                for offset, length, row, stride in pieces:
+                    res[first, middle, offset : offset + length, :] += elem[
                         pl.ds(row, length, stride=stride), :
                     ]
-        if comp < 2:
-            for side in (0, 1):
-                z = side * size[2]
-                for x in range(res.shape[0]):
-                    for y in range(res.shape[1]):
-                        packs[comp][side, x, y : y + 1, :] = res[x, y, z : z + 1, :]
-        for axis in range(3):
-            if axis == comp:
-                continue
-            for side in (0, 1):
+        rim = order[1] if comp == 0 else order[0]
+        open_size, rim_size, last_size = size[comp], size[rim], size[order[2]]
+        copies = []
+        for s_rim in (0, 1):
+            for s_last in (0, 1):
                 shift = [0, 0, 0]
-                shift[axis] = 2 * side - 1
-                if axis == 0:
-                    src = res.at[side * size[0]]
-                elif axis == 1:
-                    src = res.at[:, side * size[1]]
-                else:
-                    src = packs[comp].at[side]
-                dst = rims[comp][axis].at[side]
-                two.append(send(src, dst, shift, s2, r2, len(two)))
-        for sp in (0, 1):
-            for sr in (0, 1):
-                shift = [0, 0, 0]
-                shift[p], shift[r] = 2 * sp - 1, 2 * sr - 1
-                where = 4 * comp + 2 * sp + sr
-                if comp == 0:
-                    for x in range(size[0]):
-                        corner2[where, x : x + 1, :] = res[
-                            x, sp * size[1], sr * size[2] : sr * size[2] + 1, :
-                        ]
-                    src = corner2.at[where]
-                elif comp == 1:
-                    for y in range(size[1]):
-                        corner2[where, y : y + 1, :] = res[
-                            sp * size[0], y, sr * size[2] : sr * size[2] + 1, :
-                        ]
-                    src = corner2.at[where]
-                else:
-                    src = res.at[sp * size[0], sr * size[1]]
-                two.append(send(src, rc.at[where], shift, s2, r2, len(two)))
+                shift[rim], shift[order[2]] = 2 * s_rim - 1, 2 * s_last - 1
+                slot = 2 * s_rim + s_last
+                where = 4 * comp + slot
+                edge, row = s_rim * rim_size, s_last * last_size
+                for t in range(open_size):
+                    f, m = (t, edge) if comp == 0 else (edge, t)
+                    corner2[where, t : t + 1, :] = res[f, m, row : row + 1, :]
+                copies.append(
+                    send(corner2.at[where], rc.at[where], shift, s2, r2, 8 * comp + slot)
+                )
+        for side in (0, 1):
+            shift = [0, 0, 0]
+            shift[rim] = 2 * side - 1
+            edge = side * rim_size
+            src = res.at[:, edge] if comp == 0 else res.at[edge]
+            copies.append(send(src, near[comp].at[side], shift, s2, r2, 8 * comp + 4 + side))
+        for side in (0, 1):
+            shift = [0, 0, 0]
+            shift[order[2]] = 2 * side - 1
+            row = side * last_size
+            for f in range(res.shape[0]):
+                for m in range(res.shape[1]):
+                    packs[comp][side, f, m : m + 1, :] = res[f, m, row : row + 1, :]
+            copies.append(
+                send(packs[comp].at[side], last[comp].at[side], shift, s2, r2, 8 * comp + 6 + side)
+            )
+        sends[comp] = copies
 
     outs = (out_x, out_y, out_z)
     for comp in range(3):
         outs[comp][...] = results[comp][...]
-    for copy in two:
-        copy.wait_recv()
-    for comp in range(3):
-        out = outs[comp]
-        p, r = [t for t in range(3) if t != comp]
+    for comp in (1, 0, 2):
+        out, order = outs[comp], orders[comp]
+        rim = order[1] if comp == 0 else order[0]
+        for copy in sends[comp]:
+            copy.wait_recv()
         for side in (0, 1):
-            far = 1 - side
-            if comp != 0:
-                out[far * size[0]] += rims[comp][0][side]
-            if comp != 1:
-                for x in range(out.shape[0]):
-                    out[x, far * size[1]] += rims[comp][1][side, x]
-            if comp != 2:
-                z = far * size[2]
-                for x in range(out.shape[0]):
-                    for y in range(out.shape[1]):
-                        out[x, y, z : z + 1, :] += rims[comp][2][side, x, y : y + 1, :]
-        for sp in (0, 1):
-            for sr in (0, 1):
-                where = 4 * comp + 2 * sp + sr
-                fp, fr = (1 - sp) * size[p], (1 - sr) * size[r]
-                if comp == 0:
-                    for x in range(size[0]):
-                        out[x, fp, fr : fr + 1, :] += rc[where, x : x + 1, :]
-                elif comp == 1:
-                    for y in range(size[1]):
-                        out[fp, y, fr : fr + 1, :] += rc[where, y : y + 1, :]
-                else:
-                    out[fp, fr] += rc[where]
-    for copy in one + two:
+            edge = (1 - side) * size[rim]
+            row = (1 - side) * size[order[2]]
+            if comp == 0:
+                for f in range(out.shape[0]):
+                    out[f, edge] += near[comp][side, f]
+            else:
+                out[edge] += near[comp][side]
+            for f in range(out.shape[0]):
+                for m in range(out.shape[1]):
+                    out[f, m, row : row + 1, :] += last[comp][side, f, m : m + 1, :]
+            for s_last in (0, 1):
+                where = 4 * comp + 2 * side + s_last
+                row = (1 - s_last) * size[order[2]]
+                for t in range(size[comp]):
+                    f, m = (t, edge) if comp == 0 else (edge, t)
+                    out[f, m, row : row + 1, :] += rc[where, t : t + 1, :]
+    for copy in one + sends[0] + sends[1] + sends[2]:
         copy.wait_send()
+
+
+def write_out(from_x, from_y, from_z, to_x, to_y, to_z, sems):
+    pairs = ((from_x, to_x), (from_y, to_y), (from_z, to_z))
+    copies = [pltpu.make_async_copy(src, dst, sems.at[t]) for t, (src, dst) in enumerate(pairs)]
+    for copy in copies:
+        copy.start()
+    for copy in copies:
+        copy.wait()
 
 
 def on_device(mesh_sizes, vectors, orient_flip, reluctivity, conductivity):
@@ -408,37 +419,51 @@
     lanes = vectors.shape[-1]
     f32 = jnp.float32
     shapes = (
-        (sx, sy + 1, sz + 1, lanes), (sx + 1, sy, sz + 1, lanes), (sx + 1, sy + 1, sz, lanes),
+        (sx, sy + 1, sz + 1, lanes), (sx + 1, sy, sz + 1, lanes), (sx + 1, sz, sy + 1, lanes),
     )
     longest = max(sx, sy, sz)
+    faces = tuple((2,) + s[:2] + (lanes,) for s in shapes)
     scratch = [
         (ELEM_DOFS * ne, lanes), (ELEM_DOFS * ne, lanes), (QPTS * ne, lanes), (QPTS * ne, lanes),
         (3, ne, ELEM_DOFS), (ELEM_DOFS * ne, lanes), (3 * QPTS * ne, lanes), (3 * QPTS * ne, lanes),
         *shapes,
         (2, sx, sy, lanes), (2, longest, lanes),
         (2, sy, sz, lanes), (2, sx, sz, lanes), (2, sx, sy, lanes), (3, longest, lanes),
-        (2, sx, sy + 1, lanes), (2, sx + 1, sy, lanes), (12, longest, lanes),
-        (2, sx, sz + 1, lanes), (2, sx, sy + 1, lanes),
-        (2, sy, sz + 1, lanes), (2, sx + 1, sy, lanes),
-        (2, sy + 1, sz, lanes), (2, sx + 1, sz, lanes),
-        (12, longest, lanes),
+        *faces, (12, longest, lanes),
+        (2, sx, sz + 1, lanes), (2, sy, sz + 1, lanes), (2, sz, sy + 1, lanes),
+        *faces, (12, longest, lanes),
     ]
     vmem = pl.BlockSpec(memory_space=pltpu.VMEM)
-    return tuple(
-        pl.pallas_call(
-            functools.partial(kernel, mesh_sizes),
-            out_shape=[jax.ShapeDtypeStruct(s, f32) for s in shapes],
-            in_specs=[vmem] * 4,
-            out_specs=[vmem] * 3,
-            scratch_shapes=[pltpu.VMEM(s, f32) for s in scratch]
-            + [pltpu.SemaphoreType.DMA((7,))] * 2
-            + [pltpu.SemaphoreType.DMA((24,))] * 2,
-            compiler_params=pltpu.CompilerParams(
-                collective_id=0, has_side_effects=True, vmem_limit_bytes=48 * 2**20
-            ),
-            name="curl_mass",
-        )(vectors, orient_flip, reluctivity, conductivity)
-    )
+    padded = [s[0] * s[1] * (s[2] + -s[2] % 8) * lanes * 4 for s in shapes]
+    room = sum(padded) + max(padded)
+    anywhere = pl.BlockSpec(memory_space=pltpu.HBM)
+    arguments = (vectors, orient_flip, reluctivity, conductivity)
+    outs = [jax.ShapeDtypeStruct(s, f32) for s in shapes]
+    held = pl.pallas_call(
+        functools.partial(kernel, mesh_sizes),
+        out_shape=[pltpu.VMEM(s, f32) for s in shapes],
+        in_specs=[anywhere] * 4,
+        out_specs=[vmem] * 3,
+        scratch_shapes=[pltpu.VMEM(a.shape, a.dtype) for a in arguments]
+        + [pltpu.VMEM(s, f32) for s in scratch]
+        + [pltpu.SemaphoreType.DMA((7,))] * 2
+        + [pltpu.SemaphoreType.DMA((24,))] * 2
+        + [pltpu.SemaphoreType.DMA((4,))],
+        compiler_params=pltpu.CompilerParams(
+            collective_id=0, has_side_effects=True, vmem_limit_bytes=VMEM_ALL - room
+        ),
+        name="curl_mass",
+    )(*arguments)
+    held = pl.pallas_call(
+        write_out,
+        out_shape=outs,
+        in_specs=[pl.BlockSpec(memory_space=pl.ANY)] * 3,
+        out_specs=[anywhere] * 3,
+        scratch_shapes=[pltpu.SemaphoreType.DMA((3,))],
+        compiler_params=pltpu.CompilerParams(vmem_limit_bytes=2**20),
+        name="write_out",
+    )(*held)
+    return held[0], held[1], jnp.swapaxes(held[2], 1, 2)
 
 
 def solution(mesh):

time: 23.9 us -> 19 us (0.79)
  local copies, waits for them, and re-layouts: 5.1 us -> 0 us
  Pallas kernels: 17.9 us -> 18.2 us
    unnamed x10 -> x0, local copies, waits for them, and re-layouts: 4.4 us -> none
    pallas_call x1 -> x0, local copies, waits for them, and re-layouts: 0.7 us -> none  [on_device(): pl.pallas_call(functools.partial(kernel, mesh_sizes), out_shape=[jax.Shap...]
    pallas_call x1 -> x2, Pallas kernels: 17.9 us -> 18.2 us  [the longest x1 17.4 us: on_device(): pl.pallas_call(functools.partial(kernel, mesh_sizes), out_shape=[pltpu.VM...]
where the time goes in v1:
time: 19 us; the launch traced here: 18.8 us
  Pallas kernels  18.2 us (96%)
  between operations  0.64 us (3%)
    pallas_call x1, Pallas kernels, on_device(): pl.pallas_call(functools.partial(kernel, mesh_sizes), out_shape=[pltpu.VM...  17.4 us
    pallas_call x1, Pallas kernels, on_device(): pl.pallas_call(write_out, out_shape=outs, in_specs=[pl.BlockSpec(memory_s...  0.79 us

profile of v1, /device:TPU:0, one launch (start us, length us, event | category | flops | bytes accessed | tf_op | source)
XLA Modules:
  0.0 18.8 jit_solution(12871894629884561974)
XLA Ops:
  0.6 17.4 %curl_mass.1 = (f32[6,7,7,128]{3,2,1,0:T(8,128)S(1)}, f32[7,6,7,128]{3,2,1,0:T(8,128)S(1)}, f32[7,6,7,128]{3,2,1,0:T(8,128)S(1)}) custom-call(f32[3,6,6,6,128]{4,3,2,1,0:T(8,128)} %vec_hbm.1, s32[2,2,288]{2,1,0:T(2,128)} %flip_hbm.1, f32[2,2,128]{2,1,0:T(2,128)} %reluct_hbm.1, f32[2,2,128]{2,1,0:T(2,128)} %conduct_hbm.1), custom_call_target="tpu_custom_call" | custom-call | tf_op jit(solution)/shard_map/curl_mass/pallas_call | solution.py:442
  18.0 0.8 %write_out.1 = (f32[6,7,7,128]{3,2,1,0:T(8,128)}, f32[7,6,7,128]{3,2,1,0:T(8,128)}, f32[7,6,7,128]{3,2,1,0:T(8,128)}) custom-call(f32[6,7,7,128]{3,2,1,0:T(8,128)S(1)} %get-tuple-element.9.from_x, f32[7,6,7,128]{3,2,1,0:T(8,128)S(1)} %get-tuple-element.10.from_y, f32[7,6,7,128]{3,2,1,0:T(8,128)S(1)} %get-tuple-element.11.from_z), custom_call_target="tpu_custom_call" | custom-call | tf_op jit(solution)/shard_map/write_out/pallas_call | solution.py:457

commit v2 on v1

--- a/solution.py
+++ b/solution.py
@@ -207,20 +207,30 @@
             for y in range(size[1]):
                 put(comp, 2, (x, y, 0), 0, size[2], lambda a, b: vec[comp, x, y, a:b, :])
 
-    for copy in one:
-        copy.wait_recv()
-    for slot, comp in ((0, 0), (1, 2)):
-        for x in range(size[0]):
-            put(comp, 2, (x, size[1], 0), 0, size[2], lambda a, b: hy[slot, x, a:b, :])
-    for slot, comp in ((0, 1), (1, 2)):
-        for y in range(size[1]):
-            put(comp, 2, (size[0], y, 0), 0, size[2], lambda a, b: hx[slot, y, a:b, :])
-    for comp in (0, 1):
-        for x in range(size[0]):
-            put(comp, 1, (x, 0, size[2]), 0, size[1], lambda a, b: hz[comp, x, a:b, :])
-    put(0, 0, (0, size[1], size[2]), 0, size[0], lambda a, b: hc[0, a:b, :])
-    put(1, 1, (size[0], 0, size[2]), 0, size[1], lambda a, b: hc[1, a:b, :])
-    put(2, 2, (size[0], size[1], 0), 0, size[2], lambda a, b: hc[2, a:b, :])
+    def take_halo(comp):
+        if comp == 1:
+            for which in (2, 5, 6):
+                one[which].wait_recv()
+            for y in range(size[1]):
+                put(1, 2, (size[0], y, 0), 0, size[2], lambda a, b: hx[0, y, a:b, :])
+            for x in range(size[0]):
+                put(1, 1, (x, 0, size[2]), 0, size[1], lambda a, b: hz[1, x, a:b, :])
+            put(1, 1, (size[0], 0, size[2]), 0, size[1], lambda a, b: hc[1, a:b, :])
+        elif comp == 0:
+            for which in (0, 3):
+                one[which].wait_recv()
+            for x in range(size[0]):
+                put(0, 2, (x, size[1], 0), 0, size[2], lambda a, b: hy[0, x, a:b, :])
+                put(0, 1, (x, 0, size[2]), 0, size[1], lambda a, b: hz[0, x, a:b, :])
+            put(0, 0, (0, size[1], size[2]), 0, size[0], lambda a, b: hc[0, a:b, :])
+        else:
+            for which in (1, 4):
+                one[which].wait_recv()
+            for x in range(size[0]):
+                put(2, 2, (x, size[1], 0), 0, size[2], lambda a, b: hy[1, x, a:b, :])
+            for y in range(size[1]):
+                put(2, 2, (size[0], y, 0), 0, size[2], lambda a, b: hx[1, y, a:b, :])
+            put(2, 2, (size[0], size[1], 0), 0, size[2], lambda a, b: hc[2, a:b, :])
 
     def rows_of(axis, at, line, dims):
         others = [t for t in range(3) if t != axis]
@@ -255,7 +265,8 @@
     def mid_dims(comp):
         return [ORDER if axis == comp else QUAD for axis in range(3)]
 
-    for comp in range(3):
+    for comp in (1, 0, 2):
+        take_halo(comp)
         dims = dims_of(comp)
         base = comp * 48 * ne
         for a in range(ORDER):

time: 19 us -> 18.8 us (0.989)
  Pallas kernels: 18.2 us -> 18 us
    pallas_call x1, Pallas kernels: 17.4 us -> 17.2 us  [on_device(): pl.pallas_call(functools.partial(kernel, mesh_sizes), out_shape=[pltpu.VM...]
where the time goes in v2:
time: 18.8 us; the launch traced here: 18.6 us
  Pallas kernels  18 us (96%)
  between operations  0.64 us (3%)
    pallas_call x1, Pallas kernels, on_device(): pl.pallas_call(functools.partial(kernel, mesh_sizes), out_shape=[pltpu.VM...  17.2 us
    pallas_call x1, Pallas kernels, on_device(): pl.pallas_call(write_out, out_shape=outs, in_specs=[pl.BlockSpec(memory_s...  0.79 us

profile of v2, /device:TPU:0, one launch (start us, length us, event | category | flops | bytes accessed | tf_op | source)
XLA Modules:
  0.0 18.6 jit_solution(7885236861628514574)
XLA Ops:
  0.6 17.2 %curl_mass.1 = (f32[6,7,7,128]{3,2,1,0:T(8,128)S(1)}, f32[7,6,7,128]{3,2,1,0:T(8,128)S(1)}, f32[7,6,7,128]{3,2,1,0:T(8,128)S(1)}) custom-call(f32[3,6,6,6,128]{4,3,2,1,0:T(8,128)} %vec_hbm.1, s32[2,2,288]{2,1,0:T(2,128)} %flip_hbm.1, f32[2,2,128]{2,1,0:T(2,128)} %reluct_hbm.1, f32[2,2,128]{2,1,0:T(2,128)} %conduct_hbm.1), custom_call_target="tpu_custom_call" | custom-call | tf_op jit(solution)/shard_map/curl_mass/pallas_call | solution.py:453
  17.8 0.8 %write_out.1 = (f32[6,7,7,128]{3,2,1,0:T(8,128)}, f32[7,6,7,128]{3,2,1,0:T(8,128)}, f32[7,6,7,128]{3,2,1,0:T(8,128)}) custom-call(f32[6,7,7,128]{3,2,1,0:T(8,128)S(1)} %get-tuple-element.9.from_x, f32[7,6,7,128]{3,2,1,0:T(8,128)S(1)} %get-tuple-element.10.from_y, f32[7,6,7,128]{3,2,1,0:T(8,128)S(1)} %get-tuple-element.11.from_z), custom_call_target="tpu_custom_call" | custom-call | tf_op jit(solution)/shard_map/write_out/pallas_call | solution.py:468
